TPU v7x, 32 devices: a whole 2x2x4 slice. The times are simulated.
32 devices in a mesh: row: 4 (over y, x), col: 8 (over z, core).
Axes of the slice: x: 2, y: 2, z: 4, core: 2. Of those that a mesh axis runs over, the one named last changes fastest.
Arguments:
- fire_state: float32 [64, 192, 1024], P(None, 'row', 'col'), may hold values from -6 to 6
- fuel_class: int32 [192, 1024], P('row', 'col'), may hold values from 0 to 12
- firebreak: int32 [192, 1024], P('row', 'col'), may hold values 0 or 1
- ignition: int32 [192, 1024], P('row', 'col'), may hold values 0 or 1
- spread_rate: float32 [13, 64], replicated, may hold values from 0.03 to 0.12
- spread_rows: float32 [64, 64], replicated, may hold values from -0.375 to 0.375
- spread_cols: float32 [64, 64], replicated, may hold values from -0.375 to 0.375
- reaction: float32 [64, 64], replicated, may hold values from -0.75 to 0.75
- ignition_heat: float32 [64], replicated, may hold values from -4 to 4
Outputs:
- final_state: float32 [64, 192, 1024], P(None, 'row', 'col')
All inputs are finite; a program needn't handle non-finite values. No bound on the sum of `firebreak` or of `ignition` on one device may be relied on, other than what follows from the above.
Results may differ from a plain program's by a relative error of at most 0.0003.
Values sent between devices are 32-bit elements; how exact they have to be, the bound alone decides.
A program may use at most 64 MiB of HBM per device.

v0:
```python
import functools

import jax
import jax.numpy as jnp
from jax import lax
from jax.experimental import pallas as pl
from jax.experimental.pallas import tpu as pltpu
from jax.sharding import PartitionSpec as P

ITERS = 4
PAD = 8
BLOCK = 12
BF16, F32 = jnp.bfloat16, jnp.float32
MESH = pl.DeviceIdType.MESH


def split(x):
    high = x.astype(BF16)
    return high, (x - high.astype(F32)).astype(BF16)


def dot(a, b):
    return jnp.dot(a, b, preferred_element_type=F32)


def lanes(shape):
    return lax.broadcasted_iota(jnp.int32, shape, 1)


def rows_of(shape):
    return lax.broadcasted_iota(jnp.int32, shape, 0)


def on_diagonal(matrix):
    c = matrix.shape[0]
    turned = matrix.T
    wide = jnp.concatenate([turned, turned], axis=1)
    first = lanes(wide.shape) < c
    return jnp.concatenate([jnp.where(first, wide, 0.0), jnp.where(first, 0.0, wide)], axis=0)


def kernel(
    dims,
    x_hbm, fuel_hbm, break_hbm, lit_hbm, rate_hbm, srow_hbm, scol_hbm, react_hbm, heat_hbm,
    out_ref,
    x_ref, fuel_ref, break_ref, lit_ref, rate_ref, srow_ref, scol_ref, react_ref, heat_ref, ends_ref, load_sem,
    v, mid, local, coef, burn, heat, gr, gc, w1, w2, w3, wc, send_row, send_col, recv_row, recv_col, send_sem, recv_sem,
):
    n_row, n_col, c, h, w, k8 = dims
    p_all, half = h // 2, w // 2
    two = 2 * c
    r, q = lax.axis_index("row"), lax.axis_index("col")
    has_up, has_down = r > 0, r < n_row - 1
    has_left, has_right = q > 0, q < n_col - 1
    partner = ({"row": r - 1}, {"row": r + 1}, {"col": q - 1}, {"col": q + 1})
    sends = (has_up, has_down, has_left, has_right)
    takes = (has_down, has_up, has_right, has_left)

    def load(n, src, dst):
        return pltpu.make_async_copy(src, dst, load_sem.at[n])

    end_loads = [load(0, x_hbm.at[:, 0, :], ends_ref.at[0]), load(1, x_hbm.at[:, h - 1, :], ends_ref.at[1])]
    weight_loads = [load(2, srow_hbm, srow_ref), load(3, scol_hbm, scol_ref), load(4, react_hbm, react_ref)]
    field_load = load(5, x_hbm, x_ref.reshape(c, h, w))
    cell_loads = [
        load(6, fuel_hbm, fuel_ref), load(7, break_hbm, break_ref), load(8, lit_hbm, lit_ref),
        load(9, rate_hbm, rate_ref), load(10, heat_hbm, heat_ref),
    ]
    for one in end_loads + weight_loads + [field_load] + cell_loads:
        one.start()

    recv_row[...] = jnp.zeros_like(recv_row)
    recv_col[...] = jnp.zeros_like(recv_col)
    barrier = pltpu.get_barrier_semaphore()
    for d in range(4):
        @pl.when(sends[d])
        def _(d=d):
            pl.semaphore_signal(barrier, inc=1, device_id=partner[d], device_id_type=MESH)

    def copy(slot, d):
        src, dst = (send_row, recv_row) if d < 2 else (send_col, recv_col)
        return pltpu.make_async_remote_copy(
            src_ref=src.at[slot, d % 2],
            dst_ref=dst.at[slot, d % 2],
            send_sem=send_sem.at[slot, d],
            recv_sem=recv_sem.at[slot, d],
            device_id=partner[d],
            device_id_type=MESH,
        )

    def start(slot, d):
        @pl.when(sends[d])
        def _():
            copy(slot, d).start()

    def sent(slot):
        for d in range(4):
            @pl.when(sends[d])
            def _(d=d):
                copy(slot, d).wait_send()

    def arrived(slot):
        for d in range(4):
            @pl.when(takes[d])
            def _(d=d):
                copy(slot, d).wait_recv()

    first_half = lanes((half, two)) < c

    def send_rows(slot, top, bottom):
        send_row[slot, 0] = jnp.where(first_half, top[:half], pltpu.roll(top[half:], c, axis=1))
        send_row[slot, 1] = jnp.where(first_half, pltpu.roll(bottom[:half], c, axis=1), bottom[half:])
        odd = lax.rem(r, 2) == 1

        @pl.when(odd)
        def _():
            start(slot, 1)
            start(slot, 0)

        @pl.when(jnp.logical_not(odd))
        def _():
            start(slot, 0)
            start(slot, 1)

    def turn_in(p):
        tall = jnp.concatenate([x_ref[pl.ds(p, c, stride=h), :], x_ref[pl.ds(p + p_all, c, stride=h), :]], axis=0)
        v[p] = tall.T

    def turn_in_loop(p, carry):
        turn_in(p)
        return carry

    def column(ref, at):
        size = ref.shape[1]
        flat = ref.reshape(ref.shape[0] * size, two)
        return lambda p: flat[pl.ds(p * size + at, p_all, stride=size), :]

    def send_cols(slot, left, right):
        send_col[slot, 0] = left
        send_col[slot, 1] = right
        start(slot, 2)
        start(slot, 3)

    n_near = sum(s.astype(jnp.int32) for s in sends)
    for one in end_loads:
        one.wait()
    ends = jnp.concatenate([ends_ref[0], ends_ref[1]], axis=0).T
    pl.semaphore_wait(barrier, n_near)
    send_rows(0, ends, ends)

    for one in weight_loads:
        one.wait()
    eye = (rows_of((two, two)) == lanes((two, two))).astype(F32)
    row_hi, row_lo = split(eye + on_diagonal(srow_ref[...]))
    col_hi, col_lo = split(eye + on_diagonal(scol_ref[...]))
    rea_hi, rea_lo = split(on_diagonal(react_ref[...]))
    both_hi = jnp.concatenate([row_hi, col_hi], axis=1)
    w1[0:two] = both_hi
    w1[two:2 * two] = both_hi
    w2[...] = jnp.concatenate([row_lo, col_lo], axis=1)
    w3[0:two] = jnp.concatenate([rea_hi, rea_lo], axis=1)
    w3[two:2 * two] = jnp.concatenate([rea_hi, jnp.zeros_like(rea_lo)], axis=1)

    field_load.wait()
    lax.fori_loop(0, p_all, turn_in_loop, 0, unroll=4)
    send_cols(0, column(v, 0)(0), column(v, w - 1)(0))
    for one in cell_loads:
        one.wait()

    k = rate_ref.shape[0]
    part = k8 + 8
    rates = jnp.concatenate([rate_ref[...], rate_ref[...]], axis=1)
    heats = jnp.concatenate([heat_ref[...], heat_ref[...]], axis=1)
    wc[...] = jnp.zeros_like(wc)
    for s in range(2):
        mine = (lanes((1, two)) < c) if s == 0 else (lanes((1, two)) >= c)
        wc[s * part:s * part + k, 0:two] = jnp.where(mine, rates, 0.0)
        wc[s * part + k8:s * part + k8 + 1, two:2 * two] = jnp.where(mine, 1.0, 0.0)
        wc[s * part + k8 + 1:s * part + k8 + 2, 2 * two:3 * two] = jnp.where(mine, heats, 0.0)
    tables = jnp.concatenate(split(wc[...]), axis=0)
    classes, slots = rows_of((k8, w)), rows_of((8, w))

    def cells(p, carry):
        parts = []
        for s in range(2):
            at = pl.ds(p + s * p_all, 1)
            alive = 1.0 - break_ref[at, :].astype(F32)
            lit = alive * lit_ref[at, :].astype(F32)
            parts.append(jnp.where(fuel_ref[at, :] == classes, alive, 0.0))
            parts.append(jnp.where(slots == 0, alive, jnp.where(slots == 1, lit, 0.0)))
        tall = jnp.concatenate(parts + parts, axis=0)
        terms = dot(tall.T.astype(BF16), tables)
        coef[p] = terms[:, 0:two]
        burn[p] = terms[:, two:2 * two]
        heat[p] = terms[:, 2 * two:3 * two]
        return carry

    lax.fori_loop(0, p_all, cells, 0, unroll=4)

    def spreads(x):
        hi, lo = split(x)
        return dot(jnp.concatenate([hi, lo], axis=1), w1[...]) + dot(hi, w2[...])

    def pointwise(cur, second):
        def body(b, carry):
            at = pl.ds(b * BLOCK, BLOCK)
            x = cur[at].reshape(BLOCK * w, two)
            g = spreads(x)
            g_row, g_col = g[:, :two], g[:, two:]
            hi, lo = split(jnp.tanh(x))
            both = dot(jnp.concatenate([hi, lo], axis=1), w3[...])
            burning = both[:, :two] + both[:, two:]
            flat = lambda ref: ref[at].reshape(BLOCK * w, two)
            fire = flat(burn) * burning + flat(heat) - 2.0 * (flat(coef) * (g_row + g_col)) + 0.5 * x
            if second:
                fire = 0.5 * (fire + flat(v))
            gr[pl.ds(b * BLOCK + 1, BLOCK)] = g_row.reshape(BLOCK, w, two)
            gc[at, PAD:PAD + w] = g_col.reshape(BLOCK, w, two)
            local[at] = fire.reshape(BLOCK, w, two)
            return carry

        lax.fori_loop(0, p_all // BLOCK, body, 0)

    def halo(slot):
        stacked = jnp.concatenate([recv_row[slot, 0], recv_row[slot, 1], recv_col[slot, 0], recv_col[slot, 1]], axis=0)
        g = spreads(stacked)
        below, above = g[0:half, :two], g[half:w, :two]
        last, top = gr[p_all], gr[1]
        wide_first = lanes((w, two)) < c
        over = jnp.concatenate([above, pltpu.roll(above, c, axis=1)], axis=0)
        under = jnp.concatenate([pltpu.roll(below, c, axis=1), below], axis=0)
        gr[0] = jnp.where(wide_first, over, pltpu.roll(last, c, axis=1))
        gr[p_all + 1] = jnp.where(wide_first, pltpu.roll(top, c, axis=1), under)
        flat = gc.reshape(p_all * (w + 2 * PAD), two)
        flat[pl.ds(PAD + w, p_all, stride=w + 2 * PAD), :] = g[w:w + p_all, two:]
        flat[pl.ds(PAD - 1, p_all, stride=w + 2 * PAD), :] = g[w + p_all:w + 2 * p_all, two:]

    def combine(slot, target, second, last):
        def value(p):
            near = (gr[p] + gr[p + 2]) + (gc[p, PAD - 1:PAD - 1 + w] + gc[p, PAD + 1:PAD + 1 + w])
            if second:
                near = 0.5 * near
            return local[p] + coef[p] * near

        def edge(at):
            near = (column(gr, at)(0) + column(gr, at)(2)) + (column(gc, PAD - 1 + at)(0) + column(gc, PAD + 1 + at)(0))
            if second:
                near = 0.5 * near
            return column(local, at)(0) + column(coef, at)(0) * near

        top, bottom = value(0), value(p_all - 1)
        target[0] = top
        target[p_all - 1] = bottom

        def edges():
            send_rows(slot, top, bottom)
            send_cols(slot, edge(0), edge(w - 1))

        if last is None:
            edges()
        else:
            pl.when(jnp.logical_not(last))(edges)

        def body(p, carry):
            target[p] = value(p)
            return carry

        lax.fori_loop(1, p_all - 1, body, 0, unroll=2)

    def step(i, carry):
        pointwise(v, False)
        arrived(0)
        halo(0)
        combine(1, mid, False, None)
        pointwise(mid, True)
        arrived(1)
        halo(1)
        sent(0)
        combine(0, v, True, i == ITERS - 1)
        sent(1)
        return carry

    lax.fori_loop(0, ITERS, step, 0)

    def turn_out(p, carry):
        tall = v[p].T
        out_ref[pl.ds(p, c, stride=h), :] = tall[:c]
        out_ref[pl.ds(p + p_all, c, stride=h), :] = tall[c:]
        return carry

    lax.fori_loop(0, p_all, turn_out, 0, unroll=4)


def per_device(n_row, n_col, fire_state, fuel_class, firebreak, ignition, spread_rate, spread_rows, spread_cols, reaction, ignition_heat):
    c, h, w = fire_state.shape
    k = spread_rate.shape[0]
    k8 = -(-k // 8) * 8
    p_all, two = h // 2, 2 * c
    vmem = pl.BlockSpec(memory_space=pltpu.VMEM)
    field = pltpu.VMEM((p_all, w, two), F32)
    out = pl.pallas_call(
        functools.partial(kernel, (n_row, n_col, c, h, w, k8)),
        out_shape=jax.ShapeDtypeStruct((c * h, w), F32),
        in_specs=[pl.BlockSpec(memory_space=pltpu.HBM)] * 9,
        out_specs=vmem,
        scratch_shapes=[
            pltpu.VMEM((c * h, w), F32),
            pltpu.VMEM((h, w), jnp.int32), pltpu.VMEM((h, w), jnp.int32), pltpu.VMEM((h, w), jnp.int32),
            pltpu.VMEM(spread_rate.shape, F32),
            pltpu.VMEM((c, c), F32), pltpu.VMEM((c, c), F32), pltpu.VMEM((c, c), F32),
            pltpu.VMEM((1, c), F32),
            pltpu.VMEM((2, c, w), F32),
            pltpu.SemaphoreType.DMA((11,)),
            field, field, field, field, field, field,
            pltpu.VMEM((p_all + 2, w, two), F32),
            pltpu.VMEM((p_all, w + 2 * PAD, two), F32),
            pltpu.VMEM((2 * two, 2 * two), BF16),
            pltpu.VMEM((two, 2 * two), BF16),
            pltpu.VMEM((2 * two, 2 * two), BF16),
            pltpu.VMEM((2 * (k8 + 8), 3 * two), F32),
            pltpu.VMEM((2, 2, w // 2, two), F32),
            pltpu.VMEM((2, 2, p_all, two), F32),
            pltpu.VMEM((2, 2, w // 2, two), F32),
            pltpu.VMEM((2, 2, p_all, two), F32),
            pltpu.SemaphoreType.DMA((2, 4)),
            pltpu.SemaphoreType.DMA((2, 4)),
        ],
        compiler_params=pltpu.CompilerParams(collective_id=0, has_side_effects=True, vmem_limit_bytes=56 * 1048576),
    )(
        fire_state, fuel_class, firebreak, ignition,
        spread_rate, spread_rows, spread_cols, reaction, ignition_heat.reshape(1, c),
    )
    return out.reshape(c, h, w)


def solution(mesh):
    grid = P("row", "col")
    field = P(None, "row", "col")
    return jax.shard_map(
        functools.partial(per_device, mesh.shape["row"], mesh.shape["col"]),
        mesh=mesh,
        in_specs=(field, grid, grid, grid, P(), P(), P(), P(), P()),
        out_specs=field,
        check_vma=False,
    )
```

profile of v0, /device:TPU:1, one launch (start us, length us, event | category | flops | bytes accessed | tf_op | source)
XLA Modules:
  0.0 39.9 jit_solution(13998948854522684369)
XLA Ops:
  0.0 37.3 %shard_map.91 = f32[3072,128]{1,0:T(8,128)} custom-call(f32[64,48,128]{2,1,0:T(8,128)} %x_hbm.1, s32[48,128]{1,0:T(8,128)} %fuel_hbm.1, s32[48,128]{1,0:T(8,128)} %break_hbm.1, s32[48,128]{1,0:T(8,128)} %lit_hbm.1, f32[13,64]{1,0:T(8,128)} %rate_hbm.1, f32[64,64]{1,0:T(8,128)} %srow_hbm.1, f32[64,64]{1,0:T(8,128)} %scol_hbm.1, f32[64,64]{1,0:T(8,128)} %react_hbm.1, ...), custom_call_target="tpu_custom_call" | custom-call | tf_op jit(solution)/shard_map/pallas_call | solution.py:301
  37.3 2.7 %copy.11 = f32[64,48,128]{2,1,0:T(8,128)} copy(f32[64,48,128]{2,1,0:T(8,128)} %bitcast.2) | data formatting | bytes 3145728
where the time goes:
time: 40.6 us; the launch traced here: 39.9 us
  Pallas kernels  37.3 us (92%)
  local copies, waits for them, and re-layouts  2.65 us (7%)
    pallas_call x1, Pallas kernels, per_device(): pl.pallas_call(functools.partial(kernel, (n_row, n_col, c, h, w, k8)), ou...  37.3 us
    unnamed x1, local copies, waits for them, and re-layouts  2.65 us

commit v1 on v0

v1 whole, which is shorter than its diff:
```python
import functools

import jax
import jax.numpy as jnp
from jax import lax
from jax.experimental import pallas as pl
from jax.experimental.pallas import tpu as pltpu
from jax.sharding import PartitionSpec as P

ITERS = 4
DEPTH = 2 * ITERS
PAD = 8
BLOCK = 4
CHUNK = 4
BF16, F32 = jnp.bfloat16, jnp.float32
MESH = pl.DeviceIdType.MESH


def split(x):
    high = x.astype(BF16)
    return high, (x - high.astype(F32)).astype(BF16)


def dot(a, b):
    return jnp.dot(a, b, preferred_element_type=F32)


def lanes(shape):
    return lax.broadcasted_iota(jnp.int32, shape, 1)


def rows_of(shape):
    return lax.broadcasted_iota(jnp.int32, shape, 0)


def on_diagonal(matrix):
    c = matrix.shape[0]
    turned = matrix.T
    wide = jnp.concatenate([turned, turned], axis=1)
    first = lanes(wide.shape) < c
    return jnp.concatenate([jnp.where(first, wide, 0.0), jnp.where(first, 0.0, wide)], axis=0)


def kernel(
    dims,
    x_hbm, fuel_hbm, break_hbm, lit_hbm, rate_hbm, srow_hbm, scol_hbm, react_hbm, heat_hbm,
    out_ref,
    x_ref, fuel_ref, break_ref, lit_ref, rate_ref, srow_ref, scol_ref, react_ref, heat_ref, load_sem,
    v, mid, coef, burn, heat, ws, wa, wc, halo_x, flat_send, flat_recv,
    row_send, row_recv, int_send, int_recv, col_send, col_recv, flat_ssem, flat_rsem, corner_send, corner_recv,
):
    n_row, n_col, c, h, w, k8 = dims
    d = DEPTH
    own = h // 2
    total = own + d
    wide = w + 2 * d
    two = 2 * c
    r, q = lax.axis_index("row"), lax.axis_index("col")
    partner = ({"row": r - 1}, {"row": r + 1}, {"col": q - 1}, {"col": q + 1})
    has = (r > 0, r < n_row - 1, q > 0, q < n_col - 1)

    def load(n, src, dst):
        return pltpu.make_async_copy(src, dst, load_sem.at[n])

    body = pl.ds(d, h)
    cell_loads = [
        load(0, fuel_hbm, fuel_ref.at[body]), load(1, break_hbm, break_ref.at[body]), load(2, lit_hbm, lit_ref.at[body]),
        load(3, rate_hbm, rate_ref), load(4, heat_hbm, heat_ref),
    ]
    weight_loads = [load(5, srow_hbm, srow_ref), load(6, scol_hbm, scol_ref), load(7, react_hbm, react_ref)]
    field_load = load(8, x_hbm, x_ref.reshape(c, h, w))
    for one in [field_load] + cell_loads + weight_loads:
        one.start()

    for at in (pl.ds(0, d), pl.ds(h + d, d)):
        fuel_ref[at] = jnp.zeros((d, w), jnp.int32)
        lit_ref[at] = jnp.zeros((d, w), jnp.int32)
        break_ref[at] = jnp.ones((d, w), jnp.int32)
    flat_recv[...] = jnp.ones_like(flat_recv)
    halo_x[...] = jnp.zeros_like(halo_x)
    v[:, PAD:PAD + d] = jnp.zeros((total + 1, d, two), F32)
    v[:, PAD + d + w:PAD + wide] = jnp.zeros((total + 1, d, two), F32)

    barrier = pltpu.get_barrier_semaphore()
    for s in range(4):
        @pl.when(has[s])
        def _(s=s):
            pl.semaphore_signal(barrier, inc=1, device_id=partner[s], device_id_type=MESH)

    def remote(src, dst, send_sem, recv_sem, s):
        return pltpu.make_async_remote_copy(
            src_ref=src, dst_ref=dst, send_sem=send_sem, recv_sem=recv_sem, device_id=partner[s], device_id_type=MESH
        )

    def int_copy(n, s):
        src = (fuel_hbm, break_hbm, lit_hbm)[n]
        dst = (fuel_ref, break_ref, lit_ref)[n]
        from_row, to_row = (0, h + d) if s == 0 else (h - d, 0)
        return remote(src.at[pl.ds(from_row, d)], dst.at[pl.ds(to_row, d)], int_send.at[n, s], int_recv.at[n, s], s)

    def row_copy(j, s):
        src, at = (j, d - 1 - j) if s == 0 else (h - 1 - j, d - 1 - j)
        return remote(x_hbm.at[:, src, :], halo_x.at[s, at], row_send.at[j, s], row_recv.at[j, s], s)

    def edge(s, at):
        if s == 2:
            return v.at[at, PAD + d:PAD + 2 * d], v.at[at, PAD + d + w:PAD + wide]
        return v.at[at, PAD + w:PAD + w + d], v.at[at, PAD:PAD + d]

    def col_copy(s):
        src, dst = edge(s, pl.ds(d, own))
        return remote(src, dst, col_send.at[s - 2], col_recv.at[s - 2], s)

    def corner_copy(j, s):
        src, dst = edge(s, pl.ds(d - CHUNK * (j + 1), CHUNK))
        return remote(src, dst, corner_send.at[j, s - 2], corner_recv.at[j, s - 2], s)

    def flat_copy(s):
        return remote(flat_send.at[s - 2], flat_recv.at[s - 2], flat_ssem.at[s - 2], flat_rsem.at[s - 2], s)

    def start(make, s):
        @pl.when(has[s])
        def _():
            make(s).start()

    def sent(make, s):
        @pl.when(has[s])
        def _():
            make(s).wait_send()

    def arrived(make, s):
        @pl.when(has[s ^ 1])
        def _():
            make(s).wait_recv()

    n_near = sum(s.astype(jnp.int32) for s in has)
    pl.semaphore_wait(barrier, n_near)
    for s in range(2):
        for n in range(3):
            start(functools.partial(int_copy, n), s)
    for j in range(d):
        for s in range(2):
            start(functools.partial(row_copy, j), s)

    for one in weight_loads:
        one.wait()
    row_hi, row_lo = split(on_diagonal(srow_ref[...]))
    col_hi, col_lo = split(on_diagonal(scol_ref[...]))
    rea_hi, rea_lo = split(on_diagonal(react_ref[...]))
    ws[0:two] = jnp.concatenate([row_hi, row_lo], axis=1)
    ws[two:2 * two] = jnp.concatenate([col_hi, col_lo], axis=1)
    wa[0:two] = jnp.concatenate([rea_hi, rea_lo], axis=1)
    wa[two:2 * two] = jnp.concatenate([rea_hi, jnp.zeros_like(rea_lo)], axis=1)

    field_load.wait()

    def turn_in(i, carry):
        tall = jnp.concatenate([x_ref[pl.ds(i, c, stride=h), :], x_ref[pl.ds(h - 1 - i, c, stride=h), :]], axis=0)
        v[d + i, PAD + d:PAD + d + w] = tall.T
        return carry

    lax.fori_loop(0, own, turn_in, 0, unroll=4)
    for s in (2, 3):
        start(col_copy, s)

    for one in cell_loads:
        one.wait()
    for s in range(2):
        for n in range(3):
            arrived(functools.partial(int_copy, n), s)

    group = w // d
    lane = lanes((w, 2 * w))
    from_col = lax.rem(lane, d) + jnp.where(lane < w, 0, w - d)
    pick = jnp.where(rows_of((w, 2 * w)) == from_col, 1.0, 0.0).astype(BF16)
    ints = [ref[...].astype(F32) for ref in (fuel_ref, break_ref, lit_ref)]
    spread_out = dot(jnp.concatenate(ints, axis=0).astype(BF16), pick)
    slot = lax.rem(lanes((group, 2 * w)), w) // d
    ups = rows_of((group, 2 * w)) == slot
    downs = (group - 1) - rows_of((group, 2 * w)) == slot
    full = h + 2 * d
    for g in range(total // group):
        lines = []
        for half in range(2):
            for n in range(3):
                first = n * full + (g * group if half == 0 else full - (g + 1) * group)
                piece = jnp.where(ups if half == 0 else downs, spread_out[first:first + group], 0.0)
                lines.append(jnp.sum(piece, axis=0, keepdims=True))
        lines.append(jnp.zeros((2, 2 * w), F32))
        packed = jnp.concatenate(lines, axis=0)
        flat_send[0, g] = packed[:, :w]
        flat_send[1, g] = packed[:, w:]
    for s in (2, 3):
        start(flat_copy, s)

    k = rate_ref.shape[0]
    part = k8 + 8
    rates = jnp.concatenate([rate_ref[...], rate_ref[...]], axis=1)
    heats = jnp.concatenate([heat_ref[...], heat_ref[...]], axis=1)
    wc[...] = jnp.zeros_like(wc)
    for s in range(2):
        mine = (lanes((1, two)) < c) if s == 0 else (lanes((1, two)) >= c)
        wc[s * part:s * part + k, 0:two] = jnp.where(mine, rates, 0.0)
        wc[s * part + k8:s * part + k8 + 1, two:2 * two] = jnp.where(mine, 1.0, 0.0)
        wc[s * part + k8 + 1:s * part + k8 + 2, 2 * two:3 * two] = jnp.where(mine, heats, 0.0)
    tables = jnp.concatenate(split(wc[...]), axis=0)
    classes, slots = rows_of((k8, w)).astype(F32), rows_of((8, w))

    def terms_of(pairs):
        parts = []
        for fuel, broken, lit in pairs:
            alive = 1.0 - broken
            parts.append(jnp.where(fuel == classes, alive, 0.0))
            parts.append(jnp.where(slots == 0, alive, jnp.where(slots == 1, alive * lit, 0.0)))
        tall = jnp.concatenate(parts + parts, axis=0)
        return dot(tall.T.astype(BF16), tables)

    def cells(p, carry):
        pairs = []
        for at in (pl.ds(p, 1), pl.ds(full - 1 - p, 1)):
            pairs.append([ref[at, :].astype(F32) for ref in (fuel_ref, break_ref, lit_ref)])
        terms = terms_of(pairs)
        for n, ref in enumerate((coef, burn, heat)):
            ref[p, d:d + w] = terms[:, n * two:(n + 1) * two]
        return carry

    lax.fori_loop(0, total, cells, 0, unroll=4)

    for s in (2, 3):
        arrived(flat_copy, s)
        arrived(col_copy, s)
    for s in (2, 3):
        to = d + w if s == 2 else 0
        for g in range(total // group):
            lines = flat_recv[s - 2, g]
            terms = terms_of([[lines[3 * half + n:3 * half + n + 1] for n in range(3)] for half in range(2)])
            for n, ref in enumerate((coef, burn, heat)):
                ref[g * group:(g + 1) * group, to:to + d] = terms[:, n * two:(n + 1) * two].reshape(group, d, two)
    for s in (2, 3):
        sent(col_copy, s)

    def evaluate(p, n, second, top=False):
        cur, target = (mid, v) if second else (v, mid)
        flat = lambda value: value.reshape(n * wide, two)
        inner = slice(PAD, PAD + wide)
        at = pl.ds(p, n)
        x = flat(cur[at, inner])
        above = flat(cur[pl.ds(p - 1, n), inner])
        if top:
            turned = pltpu.roll(cur[p + n - 1, inner], c, axis=1)
            below = jnp.concatenate([flat(cur[at, inner])[wide:], turned], axis=0)
        else:
            below = flat(cur[pl.ds(p + 1, n), inner])
        left = flat(cur[at, PAD - 1:PAD - 1 + wide])
        right = flat(cur[at, PAD + 1:PAD + 1 + wide])
        twice = x + x
        vertical = (above + below) - twice
        horizontal = (left + right) - twice
        coupled = dot(jnp.concatenate([vertical.astype(BF16), horizontal.astype(BF16)], axis=1), ws[...])
        hi, lo = split(jnp.tanh(x))
        burning = dot(jnp.concatenate([hi, lo], axis=1), wa[...])
        mixed = (vertical + horizontal) + (coupled[:, :two] + coupled[:, two:])
        fire = flat(coef[at]) * mixed + flat(burn[at]) * (burning[:, :two] + burning[:, two:])
        fire = (fire + flat(heat[at])) + 0.5 * x
        if second:
            fire = 0.5 * (fire + flat(v[at, inner]))
        target[at, inner] = fire.reshape(n, wide, two)

    def pyramid(i, carry):
        for s in range(4):
            second = s % 2 == 1
            low = d + 4 * i + s + 1
            top = 2 * BLOCK - 1 - s

            def block(b, carry):
                evaluate(low + b * BLOCK, BLOCK, second)
                return carry

            lax.fori_loop(0, own // BLOCK - 2 - i, block, 0)
            evaluate(total - top, top, second, top=True)
        return carry

    lax.fori_loop(0, ITERS // 2, pyramid, 0)

    for j in range(d // CHUNK):
        for m in range(j * CHUNK, (j + 1) * CHUNK):
            for s in range(2):
                arrived(functools.partial(row_copy, m), s)
        for m in range(CHUNK):
            p = d - CHUNK * (j + 1) + m
            v[p, PAD + d:PAD + d + w] = jnp.concatenate([halo_x[1, p], halo_x[0, p]], axis=0).T
        for s in (2, 3):
            start(functools.partial(corner_copy, j), s)
        for s in (2, 3):
            sent(functools.partial(corner_copy, j), s)
            arrived(functools.partial(corner_copy, j), s)

        def zone(t, carry):
            low = d - CHUNK * (j + 1) + 2 * t
            evaluate(low + 1, CHUNK, False)
            evaluate(low + 2, CHUNK, True)
            return carry

        lax.fori_loop(0, ITERS, zone, 0)

    def turn_out(i, carry):
        tall = v[d + i, PAD + d:PAD + d + w].T
        out_ref[pl.ds(i, c, stride=h), :] = tall[:c]
        out_ref[pl.ds(h - 1 - i, c, stride=h), :] = tall[c:]
        return carry

    lax.fori_loop(0, own, turn_out, 0, unroll=4)
    for s in range(2):
        for n in range(3):
            sent(functools.partial(int_copy, n), s)
        for j in range(d):
            sent(functools.partial(row_copy, j), s)
    for s in (2, 3):
        sent(flat_copy, s)


def per_device(n_row, n_col, fire_state, fuel_class, firebreak, ignition, spread_rate, spread_rows, spread_cols, reaction, ignition_heat):
    c, h, w = fire_state.shape
    k = spread_rate.shape[0]
    k8 = -(-k // 8) * 8
    d = DEPTH
    own, two = h // 2, 2 * c
    total, wide = own + d, w + 2 * d
    groups = total * d // w
    field = pltpu.VMEM((total + 1, wide + 2 * PAD, two), F32)
    terms = pltpu.VMEM((total, wide, two), F32)
    ints = pltpu.VMEM((h + 2 * d, w), jnp.int32)
    dma = pltpu.SemaphoreType.DMA
    out = pl.pallas_call(
        functools.partial(kernel, (n_row, n_col, c, h, w, k8)),
        out_shape=jax.ShapeDtypeStruct((c * h, w), F32),
        in_specs=[pl.BlockSpec(memory_space=pltpu.HBM)] * 9,
        out_specs=pl.BlockSpec(memory_space=pltpu.VMEM),
        scratch_shapes=[
            pltpu.VMEM((c * h, w), F32),
            ints, ints, ints,
            pltpu.VMEM(spread_rate.shape, F32),
            pltpu.VMEM((c, c), F32), pltpu.VMEM((c, c), F32), pltpu.VMEM((c, c), F32),
            pltpu.VMEM((1, c), F32),
            dma((9,)),
            field, field, terms, terms, terms,
            pltpu.VMEM((2 * two, 2 * two), BF16),
            pltpu.VMEM((2 * two, 2 * two), BF16),
            pltpu.VMEM((2 * (k8 + 8), 3 * two), F32),
            pltpu.VMEM((2, d, c, w), F32),
            pltpu.VMEM((2, groups, 8, w), F32),
            pltpu.VMEM((2, groups, 8, w), F32),
            dma((d, 2)), dma((d, 2)), dma((3, 2)), dma((3, 2)), dma((2,)), dma((2,)), dma((2,)), dma((2,)),
            dma((d // CHUNK, 2)), dma((d // CHUNK, 2)),
        ],
        compiler_params=pltpu.CompilerParams(collective_id=0, has_side_effects=True, vmem_limit_bytes=56 * 1048576),
    )(
        fire_state, fuel_class, firebreak, ignition,
        spread_rate, spread_rows, spread_cols, reaction, ignition_heat.reshape(1, c),
    )
    return out.reshape(c, h, w)


def solution(mesh):
    grid = P("row", "col")
    field = P(None, "row", "col")
    return jax.shard_map(
        functools.partial(per_device, mesh.shape["row"], mesh.shape["col"]),
        mesh=mesh,
        in_specs=(field, grid, grid, grid, P(), P(), P(), P(), P()),
        out_specs=field,
        check_vma=False,
    )
```

time: 40.6 us -> 38.6 us (0.951); the launches traced: 39.9 us -> 38.4 us
  Pallas kernels: 37.3 us -> 35.8 us
    pallas_call x1, Pallas kernels: 37.3 us -> 35.8 us  [per_device(): pl.pallas_call(functools.partial(kernel, (n_row, n_col, c, h, w, k8)), ou...]
where the time goes in v1:
time: 38.6 us; the launch traced here: 38.4 us
  Pallas kernels  35.8 us (93%)
  local copies, waits for them, and re-layouts  2.65 us (7%)
    pallas_call x1, Pallas kernels, per_device(): pl.pallas_call(functools.partial(kernel, (n_row, n_col, c, h, w, k8)), ou...  35.8 us
    unnamed x1, local copies, waits for them, and re-layouts  2.65 us

profile of v1, /device:TPU:1, one launch (start us, length us, event | category | flops | bytes accessed | tf_op | source)
XLA Modules:
  0.0 38.4 jit_solution(3948466436333118863)
XLA Ops:
  0.0 35.8 %shard_map.91 = f32[3072,128]{1,0:T(8,128)} custom-call(f32[64,48,128]{2,1,0:T(8,128)} %x_hbm.1, s32[48,128]{1,0:T(8,128)} %fuel_hbm.1, s32[48,128]{1,0:T(8,128)} %break_hbm.1, s32[48,128]{1,0:T(8,128)} %lit_hbm.1, f32[13,64]{1,0:T(8,128)} %rate_hbm.1, f32[64,64]{1,0:T(8,128)} %srow_hbm.1, f32[64,64]{1,0:T(8,128)} %scol_hbm.1, f32[64,64]{1,0:T(8,128)} %react_hbm.1, ...), custom_call_target="tpu_custom_call" | custom-call | tf_op jit(solution)/shard_map/pallas_call | solution.py:334
  35.8 2.7 %copy.11 = f32[64,48,128]{2,1,0:T(8,128)} copy(f32[64,48,128]{2,1,0:T(8,128)} %bitcast.2) | data formatting | bytes 3145728

commit v2 on v1

--- a/solution.py
+++ b/solution.py
@@ -10,7 +10,7 @@
 ITERS = 4
 DEPTH = 2 * ITERS
 PAD = 8
-BLOCK = 4
+LARGEST = 6
 CHUNK = 4
 BF16, F32 = jnp.bfloat16, jnp.float32
 MESH = pl.DeviceIdType.MESH
@@ -52,9 +52,13 @@
     n_row, n_col, c, h, w, k8 = dims
     d = DEPTH
     own = h // 2
+    half_rows = own // 2
     total = own + d
     wide = w + 2 * d
     two = 2 * c
+    group = w // d
+    groups = total // group
+    full = h + 2 * d
     r, q = lax.axis_index("row"), lax.axis_index("col")
     partner = ({"row": r - 1}, {"row": r + 1}, {"col": q - 1}, {"col": q + 1})
     has = (r > 0, r < n_row - 1, q > 0, q < n_col - 1)
@@ -107,16 +111,18 @@
             return v.at[at, PAD + d:PAD + 2 * d], v.at[at, PAD + d + w:PAD + wide]
         return v.at[at, PAD + w:PAD + w + d], v.at[at, PAD:PAD + d]
 
-    def col_copy(s):
-        src, dst = edge(s, pl.ds(d, own))
-        return remote(src, dst, col_send.at[s - 2], col_recv.at[s - 2], s)
+    def col_copy(m, s):
+        src, dst = edge(s, pl.ds(d + m * half_rows, half_rows))
+        return remote(src, dst, col_send.at[m, s - 2], col_recv.at[m, s - 2], s)
 
     def corner_copy(j, s):
         src, dst = edge(s, pl.ds(d - CHUNK * (j + 1), CHUNK))
         return remote(src, dst, corner_send.at[j, s - 2], corner_recv.at[j, s - 2], s)
 
-    def flat_copy(s):
-        return remote(flat_send.at[s - 2], flat_recv.at[s - 2], flat_ssem.at[s - 2], flat_rsem.at[s - 2], s)
+    def flat_copy(late, s):
+        at = pl.ds(groups, 1) if late else pl.ds(0, groups)
+        src, dst = flat_send.at[s - 2, at], flat_recv.at[s - 2, at]
+        return remote(src, dst, flat_ssem.at[late, s - 2], flat_rsem.at[late, s - 2], s)
 
     def start(make, s):
         @pl.when(has[s])
@@ -152,6 +158,38 @@
     wa[0:two] = jnp.concatenate([rea_hi, rea_lo], axis=1)
     wa[two:2 * two] = jnp.concatenate([rea_hi, jnp.zeros_like(rea_lo)], axis=1)
 
+    for one in cell_loads:
+        one.wait()
+
+    lane = lanes((w, 2 * w))
+    from_col = lax.rem(lane, d) + jnp.where(lane < w, 0, w - d)
+    pick = jnp.where(rows_of((w, 2 * w)) == from_col, 1.0, 0.0).astype(BF16)
+    slot = lax.rem(lanes((group, 2 * w)), w) // d
+    ups = rows_of((group, 2 * w)) == slot
+    downs = (group - 1) - rows_of((group, 2 * w)) == slot
+
+    def flatten(tall, size, blocks):
+        spread_out = dot(tall.astype(BF16), pick)
+        for to, g in blocks:
+            lines = []
+            for half in range(2):
+                for n in range(3):
+                    first = n * size + (g * group if half == 0 else size - (g + 1) * group)
+                    piece = jnp.where(ups if half == 0 else downs, spread_out[first:first + group], 0.0)
+                    lines.append(jnp.sum(piece, axis=0, keepdims=True))
+            lines.append(jnp.zeros((2, 2 * w), F32))
+            packed = jnp.concatenate(lines, axis=0)
+            flat_send[0, to] = packed[:, :w]
+            flat_send[1, to] = packed[:, w:]
+
+    fill = jnp.zeros((d, w), F32)
+    early = []
+    for ref in (fuel_ref, break_ref, lit_ref):
+        early += [fill, ref[d:d + h].astype(F32), fill]
+    flatten(jnp.concatenate(early, axis=0), full, [(g, g) for g in range(groups)])
+    for s in (2, 3):
+        start(functools.partial(flat_copy, 0), s)
+
     field_load.wait()
 
     def turn_in(i, carry):
@@ -159,39 +197,10 @@
         v[d + i, PAD + d:PAD + d + w] = tall.T
         return carry
 
-    lax.fori_loop(0, own, turn_in, 0, unroll=4)
-    for s in (2, 3):
-        start(col_copy, s)
-
-    for one in cell_loads:
-        one.wait()
-    for s in range(2):
-        for n in range(3):
-            arrived(functools.partial(int_copy, n), s)
-
-    group = w // d
-    lane = lanes((w, 2 * w))
-    from_col = lax.rem(lane, d) + jnp.where(lane < w, 0, w - d)
-    pick = jnp.where(rows_of((w, 2 * w)) == from_col, 1.0, 0.0).astype(BF16)
-    ints = [ref[...].astype(F32) for ref in (fuel_ref, break_ref, lit_ref)]
-    spread_out = dot(jnp.concatenate(ints, axis=0).astype(BF16), pick)
-    slot = lax.rem(lanes((group, 2 * w)), w) // d
-    ups = rows_of((group, 2 * w)) == slot
-    downs = (group - 1) - rows_of((group, 2 * w)) == slot
-    full = h + 2 * d
-    for g in range(total // group):
-        lines = []
-        for half in range(2):
-            for n in range(3):
-                first = n * full + (g * group if half == 0 else full - (g + 1) * group)
-                piece = jnp.where(ups if half == 0 else downs, spread_out[first:first + group], 0.0)
-                lines.append(jnp.sum(piece, axis=0, keepdims=True))
-        lines.append(jnp.zeros((2, 2 * w), F32))
-        packed = jnp.concatenate(lines, axis=0)
-        flat_send[0, g] = packed[:, :w]
-        flat_send[1, g] = packed[:, w:]
-    for s in (2, 3):
-        start(flat_copy, s)
+    for m in range(2):
+        lax.fori_loop(m * half_rows, (m + 1) * half_rows, turn_in, 0, unroll=half_rows // 2)
+        for s in (2, 3):
+            start(functools.partial(col_copy, m), s)
 
     k = rate_ref.shape[0]
     part = k8 + 8
@@ -224,20 +233,35 @@
             ref[p, d:d + w] = terms[:, n * two:(n + 1) * two]
         return carry
 
-    lax.fori_loop(0, total, cells, 0, unroll=4)
-
+    lax.fori_loop(d, total, cells, 0, unroll=4)
+
+    for s in range(2):
+        for n in range(3):
+            arrived(functools.partial(int_copy, n), s)
+    late = []
+    for ref in (fuel_ref, break_ref, lit_ref):
+        late += [ref[0:group].astype(F32), ref[full - group:full].astype(F32)]
+    flatten(jnp.concatenate(late, axis=0), 2 * group, [(groups, 0)])
     for s in (2, 3):
-        arrived(flat_copy, s)
-        arrived(col_copy, s)
+        start(functools.partial(flat_copy, 1), s)
+    lax.fori_loop(0, d, cells, 0, unroll=4)
+
+    def edge_cells(blocks):
+        for s in (2, 3):
+            to = d + w if s == 2 else 0
+            for g, source in blocks:
+                lines = flat_recv[s - 2, source]
+                terms = terms_of([[lines[3 * half + n:3 * half + n + 1] for n in range(3)] for half in range(2)])
+                for n, ref in enumerate((coef, burn, heat)):
+                    ref[g * group:(g + 1) * group, to:to + d] = terms[:, n * two:(n + 1) * two].reshape(group, d, two)
+
     for s in (2, 3):
-        to = d + w if s == 2 else 0
-        for g in range(total // group):
-            lines = flat_recv[s - 2, g]
-            terms = terms_of([[lines[3 * half + n:3 * half + n + 1] for n in range(3)] for half in range(2)])
-            for n, ref in enumerate((coef, burn, heat)):
-                ref[g * group:(g + 1) * group, to:to + d] = terms[:, n * two:(n + 1) * two].reshape(group, d, two)
-    for s in (2, 3):
-        sent(col_copy, s)
+        arrived(functools.partial(flat_copy, 0), s)
+    edge_cells([(g, g) for g in range(groups)])
+    for m in range(2):
+        for s in (2, 3):
+            arrived(functools.partial(col_copy, m), s)
+            sent(functools.partial(col_copy, m), s)
 
     def evaluate(p, n, second, top=False):
         cur, target = (mid, v) if second else (v, mid)
@@ -266,23 +290,14 @@
             fire = 0.5 * (fire + flat(v[at, inner]))
         target[at, inner] = fire.reshape(n, wide, two)
 
-    def pyramid(i, carry):
-        for s in range(4):
-            second = s % 2 == 1
-            low = d + 4 * i + s + 1
-            top = 2 * BLOCK - 1 - s
-
-            def block(b, carry):
-                evaluate(low + b * BLOCK, BLOCK, second)
-                return carry
-
-            lax.fori_loop(0, own // BLOCK - 2 - i, block, 0)
-            evaluate(total - top, top, second, top=True)
-        return carry
-
-    lax.fori_loop(0, ITERS // 2, pyramid, 0)
-
-    for j in range(d // CHUNK):
+    def pyramid(k):
+        low, count = d + k, own - k
+        blocks = -(-count // LARGEST)
+        for b in range(blocks):
+            begin, end = count * b // blocks, count * (b + 1) // blocks
+            evaluate(low + begin, end - begin, k % 2 == 0, top=b == blocks - 1)
+
+    def take_rows(j):
         for m in range(j * CHUNK, (j + 1) * CHUNK):
             for s in range(2):
                 arrived(functools.partial(row_copy, m), s)
@@ -291,17 +306,30 @@
             v[p, PAD + d:PAD + d + w] = jnp.concatenate([halo_x[1, p], halo_x[0, p]], axis=0).T
         for s in (2, 3):
             start(functools.partial(corner_copy, j), s)
+
+    def zone(j):
         for s in (2, 3):
             sent(functools.partial(corner_copy, j), s)
             arrived(functools.partial(corner_copy, j), s)
 
-        def zone(t, carry):
+        def step(t, carry):
             low = d - CHUNK * (j + 1) + 2 * t
             evaluate(low + 1, CHUNK, False)
             evaluate(low + 2, CHUNK, True)
             return carry
 
-        lax.fori_loop(0, ITERS, zone, 0)
+        lax.fori_loop(0, ITERS, step, 0)
+
+    for k in range(1, 5):
+        pyramid(k)
+    take_rows(0)
+    for k in range(5, 9):
+        pyramid(k)
+    for s in (2, 3):
+        arrived(functools.partial(flat_copy, 1), s)
+    edge_cells([(0, groups)])
+    zone(0)
+    take_rows(1)
 
     def turn_out(i, carry):
         tall = v[d + i, PAD + d:PAD + d + w].T
@@ -309,14 +337,17 @@
         out_ref[pl.ds(h - 1 - i, c, stride=h), :] = tall[c:]
         return carry
 
-    lax.fori_loop(0, own, turn_out, 0, unroll=4)
+    lax.fori_loop(d, own, turn_out, 0, unroll=8)
+    zone(1)
+    lax.fori_loop(0, d, turn_out, 0, unroll=8)
     for s in range(2):
         for n in range(3):
             sent(functools.partial(int_copy, n), s)
         for j in range(d):
             sent(functools.partial(row_copy, j), s)
     for s in (2, 3):
-        sent(flat_copy, s)
+        for late in range(2):
+            sent(functools.partial(flat_copy, late), s)
 
 
 def per_device(n_row, n_col, fire_state, fuel_class, firebreak, ignition, spread_rate, spread_rows, spread_cols, reaction, ignition_heat):
@@ -333,7 +364,7 @@
     dma = pltpu.SemaphoreType.DMA
     out = pl.pallas_call(
         functools.partial(kernel, (n_row, n_col, c, h, w, k8)),
-        out_shape=jax.ShapeDtypeStruct((c * h, w), F32),
+        out_shape=pltpu.VMEM((c * h, w), F32),
         in_specs=[pl.BlockSpec(memory_space=pltpu.HBM)] * 9,
         out_specs=pl.BlockSpec(memory_space=pltpu.VMEM),
         scratch_shapes=[
@@ -348,9 +379,9 @@
             pltpu.VMEM((2 * two, 2 * two), BF16),
             pltpu.VMEM((2 * (k8 + 8), 3 * two), F32),
             pltpu.VMEM((2, d, c, w), F32),
-            pltpu.VMEM((2, groups, 8, w), F32),
-            pltpu.VMEM((2, groups, 8, w), F32),
-            dma((d, 2)), dma((d, 2)), dma((3, 2)), dma((3, 2)), dma((2,)), dma((2,)), dma((2,)), dma((2,)),
+            pltpu.VMEM((2, groups + 1, 8, w), F32),
+            pltpu.VMEM((2, groups + 1, 8, w), F32),
+            dma((d, 2)), dma((d, 2)), dma((3, 2)), dma((3, 2)), dma((2, 2)), dma((2, 2)), dma((2, 2)), dma((2, 2)),
             dma((d // CHUNK, 2)), dma((d // CHUNK, 2)),
         ],
         compiler_params=pltpu.CompilerParams(collective_id=0, has_side_effects=True, vmem_limit_bytes=56 * 1048576),

time: 38.6 us -> 26.9 us (0.70)
  Pallas kernels: 35.8 us -> 25.6 us
  local copies, waits for them, and re-layouts: 2.65 us -> 1.15 us
    pallas_call x1, Pallas kernels: 35.8 us -> 25.6 us  [per_device(): pl.pallas_call(functools.partial(kernel, (n_row, n_col, c, h, w, k8)), ou...]
    unnamed x1, local copies, waits for them, and re-layouts: 2.65 us -> 1.15 us
where the time goes in v2:
time: 26.9 us; the launch traced here: 26.7 us
  Pallas kernels  25.6 us (95%)
  local copies, waits for them, and re-layouts  1.15 us (4%)
    pallas_call x1, Pallas kernels, per_device(): pl.pallas_call(functools.partial(kernel, (n_row, n_col, c, h, w, k8)), ou...  25.6 us
    unnamed x1, local copies, waits for them, and re-layouts  1.15 us

profile of v2, /device:TPU:1, one launch (start us, length us, event | category | flops | bytes accessed | tf_op | source)
XLA Modules:
  0.0 26.7 jit_solution(13005261411598571694)
XLA Ops:
  0.0 25.6 %shard_map.91 = f32[3072,128]{1,0:T(8,128)S(1)} custom-call(f32[64,48,128]{2,1,0:T(8,128)} %x_hbm.1, s32[48,128]{1,0:T(8,128)} %fuel_hbm.1, s32[48,128]{1,0:T(8,128)} %break_hbm.1, s32[48,128]{1,0:T(8,128)} %lit_hbm.1, f32[13,64]{1,0:T(8,128)} %rate_hbm.1, f32[64,64]{1,0:T(8,128)} %srow_hbm.1, f32[64,64]{1,0:T(8,128)} %scol_hbm.1, f32[64,64]{1,0:T(8,128)} %react_hbm.1, ...), custom_call_target="tpu_custom_call" | custom-call | tf_op jit(solution)/shard_map/pallas_call | solution.py:365
  25.6 1.1 %copy.11 = f32[64,48,128]{2,1,0:T(8,128)} copy(f32[64,48,128]{2,1,0:T(8,128)S(1)} %bitcast.2) | data formatting | bytes 3145728

commit v3 on v2

--- a/solution.py
+++ b/solution.py
@@ -10,9 +10,12 @@
 ITERS = 4
 DEPTH = 2 * ITERS
 PAD = 8
-LARGEST = 6
+TILE = 8
+LARGEST = 72
+EARLY = 3
 CHUNK = 4
 BF16, F32 = jnp.bfloat16, jnp.float32
+ROUND = 1.5 * 2.0 ** 15
 MESH = pl.DeviceIdType.MESH
 
 
@@ -23,6 +26,10 @@
 
 def dot(a, b):
     return jnp.dot(a, b, preferred_element_type=F32)
+
+
+def mixed_dot(a, b):
+    return lax.dot_general(a, b, (((1,), (0,)), ((), ())), preferred_element_type=F32)
 
 
 def lanes(shape):
@@ -46,13 +53,13 @@
     x_hbm, fuel_hbm, break_hbm, lit_hbm, rate_hbm, srow_hbm, scol_hbm, react_hbm, heat_hbm,
     out_ref,
     x_ref, fuel_ref, break_ref, lit_ref, rate_ref, srow_ref, scol_ref, react_ref, heat_ref, load_sem,
-    v, mid, coef, burn, heat, ws, wa, wc, halo_x, flat_send, flat_recv,
+    v, mid, coef, burn, heat, ws, wa, wc, halo_x, relay_x, flat_send, flat_recv,
     row_send, row_recv, int_send, int_recv, col_send, col_recv, flat_ssem, flat_rsem, corner_send, corner_recv,
+    relay_send, relay_recv,
 ):
     n_row, n_col, c, h, w, k8 = dims
     d = DEPTH
     own = h // 2
-    half_rows = own // 2
     total = own + d
     wide = w + 2 * d
     two = 2 * c
@@ -60,8 +67,9 @@
     groups = total // group
     full = h + 2 * d
     r, q = lax.axis_index("row"), lax.axis_index("col")
-    partner = ({"row": r - 1}, {"row": r + 1}, {"col": q - 1}, {"col": q + 1})
-    has = (r > 0, r < n_row - 1, q > 0, q < n_col - 1)
+    odd = lax.rem(r, 2) == 1
+    partner = ({"row": r - 1}, {"row": r + 1}, {"col": q - 1}, {"col": q + 1}, {"row": r - 2}, {"row": r + 2})
+    has = (r > 0, r < n_row - 1, q > 0, q < n_col - 1, r > 1, r < n_row - 2)
 
     def load(n, src, dst):
         return pltpu.make_async_copy(src, dst, load_sem.at[n])
@@ -72,7 +80,8 @@
         load(3, rate_hbm, rate_ref), load(4, heat_hbm, heat_ref),
     ]
     weight_loads = [load(5, srow_hbm, srow_ref), load(6, scol_hbm, scol_ref), load(7, react_hbm, react_ref)]
-    field_load = load(8, x_hbm, x_ref.reshape(c, h, w))
+    x_rows = x_ref.reshape(c, h, w)
+    field_load = load(8, x_hbm, x_rows)
     for one in [field_load] + cell_loads + weight_loads:
         one.start()
 
@@ -86,7 +95,7 @@
     v[:, PAD + d + w:PAD + wide] = jnp.zeros((total + 1, d, two), F32)
 
     barrier = pltpu.get_barrier_semaphore()
-    for s in range(4):
+    for s in range(6):
         @pl.when(has[s])
         def _(s=s):
             pl.semaphore_signal(barrier, inc=1, device_id=partner[s], device_id_type=MESH)
@@ -106,13 +115,49 @@
         src, at = (j, d - 1 - j) if s == 0 else (h - 1 - j, d - 1 - j)
         return remote(x_hbm.at[:, src, :], halo_x.at[s, at], row_send.at[j, s], row_recv.at[j, s], s)
 
+    detour = (jnp.logical_and(jnp.logical_not(odd), has[4]), jnp.logical_and(odd, has[5]))
+    relays = (jnp.logical_and(jnp.logical_not(odd), has[5]), jnp.logical_and(odd, has[4]))
+
+    def detour_copy(j, s):
+        src = j if s == 0 else h - 1 - j
+        at = j - CHUNK
+        return remote(x_hbm.at[:, src, :], relay_x.at[at], row_send.at[j, s], relay_recv.at[at], s + 4)
+
+    def relay_copy(j, s):
+        at = j - CHUNK
+        return remote(relay_x.at[at], halo_x.at[s, d - 1 - j], relay_send.at[at], row_recv.at[j, s], 1 - s)
+
+    def start_far(j, s):
+        @pl.when(jnp.logical_and(has[s], jnp.logical_not(detour[s])))
+        def _():
+            row_copy(j, s).start()
+
+        @pl.when(detour[s])
+        def _():
+            detour_copy(j, s).start()
+
+    def relay():
+        for s in range(2):
+            @pl.when(relays[s])
+            def _(s=s):
+                for j in range(CHUNK, d):
+                    detour_copy(j, s).wait_recv()
+                    relay_copy(j, s).start()
+
+    def relayed():
+        for s in range(2):
+            @pl.when(relays[s])
+            def _(s=s):
+                for j in range(CHUNK, d):
+                    relay_copy(j, s).wait_send()
+
     def edge(s, at):
         if s == 2:
             return v.at[at, PAD + d:PAD + 2 * d], v.at[at, PAD + d + w:PAD + wide]
         return v.at[at, PAD + w:PAD + w + d], v.at[at, PAD:PAD + d]
 
     def col_copy(m, s):
-        src, dst = edge(s, pl.ds(d + m * half_rows, half_rows))
+        src, dst = edge(s, pl.ds(d + m * TILE, TILE))
         return remote(src, dst, col_send.at[m, s - 2], col_recv.at[m, s - 2], s)
 
     def corner_copy(j, s):
@@ -146,7 +191,18 @@
             start(functools.partial(int_copy, n), s)
     for j in range(d):
         for s in range(2):
-            start(functools.partial(row_copy, j), s)
+            if j < CHUNK:
+                start(functools.partial(row_copy, j), s)
+            else:
+                start_far(j, s)
+
+    field_load.wait()
+    for m in range(own // TILE):
+        for i in range(m * TILE, (m + 1) * TILE):
+            tall = jnp.concatenate([x_ref[pl.ds(i, c, stride=h), :], x_ref[pl.ds(h - 1 - i, c, stride=h), :]], axis=0)
+            v[d + i, PAD + d:PAD + d + w] = tall.T
+        for s in (2, 3):
+            start(functools.partial(col_copy, m), s)
 
     for one in weight_loads:
         one.wait()
@@ -190,18 +246,6 @@
     for s in (2, 3):
         start(functools.partial(flat_copy, 0), s)
 
-    field_load.wait()
-
-    def turn_in(i, carry):
-        tall = jnp.concatenate([x_ref[pl.ds(i, c, stride=h), :], x_ref[pl.ds(h - 1 - i, c, stride=h), :]], axis=0)
-        v[d + i, PAD + d:PAD + d + w] = tall.T
-        return carry
-
-    for m in range(2):
-        lax.fori_loop(m * half_rows, (m + 1) * half_rows, turn_in, 0, unroll=half_rows // 2)
-        for s in (2, 3):
-            start(functools.partial(col_copy, m), s)
-
     k = rate_ref.shape[0]
     part = k8 + 8
     rates = jnp.concatenate([rate_ref[...], rate_ref[...]], axis=1)
@@ -235,17 +279,6 @@
 
     lax.fori_loop(d, total, cells, 0, unroll=4)
 
-    for s in range(2):
-        for n in range(3):
-            arrived(functools.partial(int_copy, n), s)
-    late = []
-    for ref in (fuel_ref, break_ref, lit_ref):
-        late += [ref[0:group].astype(F32), ref[full - group:full].astype(F32)]
-    flatten(jnp.concatenate(late, axis=0), 2 * group, [(groups, 0)])
-    for s in (2, 3):
-        start(functools.partial(flat_copy, 1), s)
-    lax.fori_loop(0, d, cells, 0, unroll=4)
-
     def edge_cells(blocks):
         for s in (2, 3):
             to = d + w if s == 2 else 0
@@ -255,47 +288,65 @@
                 for n, ref in enumerate((coef, burn, heat)):
                     ref[g * group:(g + 1) * group, to:to + d] = terms[:, n * two:(n + 1) * two].reshape(group, d, two)
 
-    for s in (2, 3):
-        arrived(functools.partial(flat_copy, 0), s)
-    edge_cells([(g, g) for g in range(groups)])
-    for m in range(2):
-        for s in (2, 3):
-            arrived(functools.partial(col_copy, m), s)
-            sent(functools.partial(col_copy, m), s)
-
-    def evaluate(p, n, second, top=False):
+    def take_cols():
+        for s in (2, 3):
+            arrived(functools.partial(flat_copy, 0), s)
+        edge_cells([(g, g) for g in range(groups)])
+        for m in range(own // TILE):
+            for s in (2, 3):
+                arrived(functools.partial(col_copy, m), s)
+
+    tiles = wide // TILE
+
+    def evaluate(p, n, second, first=0, last=tiles, top=False):
         cur, target = (mid, v) if second else (v, mid)
-        flat = lambda value: value.reshape(n * wide, two)
-        inner = slice(PAD, PAD + wide)
+        size = (last - first) * TILE
+        flat = lambda value: value.reshape(n * size, two)
+        side = lambda shift: slice(PAD + first * TILE + shift, PAD + last * TILE + shift)
+        inner, cell = side(0), side(-PAD)
         at = pl.ds(p, n)
         x = flat(cur[at, inner])
         above = flat(cur[pl.ds(p - 1, n), inner])
         if top:
             turned = pltpu.roll(cur[p + n - 1, inner], c, axis=1)
-            below = jnp.concatenate([flat(cur[at, inner])[wide:], turned], axis=0)
+            below = jnp.concatenate([x[size:], turned], axis=0) if n > 1 else turned
         else:
             below = flat(cur[pl.ds(p + 1, n), inner])
-        left = flat(cur[at, PAD - 1:PAD - 1 + wide])
-        right = flat(cur[at, PAD + 1:PAD + 1 + wide])
+        left, right = flat(cur[at, side(-1)]), flat(cur[at, side(1)])
         twice = x + x
         vertical = (above + below) - twice
         horizontal = (left + right) - twice
-        coupled = dot(jnp.concatenate([vertical.astype(BF16), horizontal.astype(BF16)], axis=1), ws[...])
-        hi, lo = split(jnp.tanh(x))
-        burning = dot(jnp.concatenate([hi, lo], axis=1), wa[...])
+        coupled = mixed_dot(jnp.concatenate([vertical, horizontal], axis=1), ws[...])
+        burnt = jnp.tanh(x)
+        hi = (burnt + ROUND) - ROUND
+        burning = mixed_dot(jnp.concatenate([hi, burnt - hi], axis=1), wa[...])
         mixed = (vertical + horizontal) + (coupled[:, :two] + coupled[:, two:])
-        fire = flat(coef[at]) * mixed + flat(burn[at]) * (burning[:, :two] + burning[:, two:])
-        fire = (fire + flat(heat[at])) + 0.5 * x
+        fire = flat(coef[at, cell]) * mixed + flat(burn[at, cell]) * (burning[:, :two] + burning[:, two:])
+        fire = (fire + flat(heat[at, cell])) + 0.5 * x
         if second:
             fire = 0.5 * (fire + flat(v[at, inner]))
-        target[at, inner] = fire.reshape(n, wide, two)
-
-    def pyramid(k):
+        target[at, inner] = fire.reshape(n, size, two)
+
+    def pyramid(k, first=0, last=tiles):
+        if k == d:
+            first, last = max(first, 1), min(last, tiles - 1)
         low, count = d + k, own - k
-        blocks = -(-count // LARGEST)
+        blocks = -(-count * (last - first) // LARGEST)
         for b in range(blocks):
             begin, end = count * b // blocks, count * (b + 1) // blocks
-            evaluate(low + begin, end - begin, k % 2 == 0, top=b == blocks - 1)
+            evaluate(low + begin, end - begin, k % 2 == 0, first, last, top=b == blocks - 1)
+
+    def take_ints():
+        for s in range(2):
+            for n in range(3):
+                arrived(functools.partial(int_copy, n), s)
+        late = []
+        for ref in (fuel_ref, break_ref, lit_ref):
+            late += [ref[0:group].astype(F32), ref[full - group:full].astype(F32)]
+        flatten(jnp.concatenate(late, axis=0), 2 * group, [(groups, 0)])
+        for s in (2, 3):
+            start(functools.partial(flat_copy, 1), s)
+        lax.fori_loop(0, d, cells, 0, unroll=4)
 
     def take_rows(j):
         for m in range(j * CHUNK, (j + 1) * CHUNK):
@@ -307,39 +358,46 @@
         for s in (2, 3):
             start(functools.partial(corner_copy, j), s)
 
+    def turn_out(i):
+        tall = v[d + i, PAD + d:PAD + d + w].T
+        out_ref[pl.ds(i, c, stride=h), :] = tall[:c]
+        out_ref[pl.ds(h - 1 - i, c, stride=h), :] = tall[c:]
+
     def zone(j):
         for s in (2, 3):
             sent(functools.partial(corner_copy, j), s)
             arrived(functools.partial(corner_copy, j), s)
-
-        def step(t, carry):
-            low = d - CHUNK * (j + 1) + 2 * t
-            evaluate(low + 1, CHUNK, False)
-            evaluate(low + 2, CHUNK, True)
-            return carry
-
-        lax.fori_loop(0, ITERS, step, 0)
-
-    for k in range(1, 5):
+        if j == 1:
+            for i in range(d, own):
+                turn_out(i)
+
+        for k in range(1, d + 1):
+            edge_tile = 1 if k == d else 0
+            evaluate(d - CHUNK * (j + 1) + k, CHUNK, k % 2 == 0, edge_tile, tiles - edge_tile)
+
+    for k in range(1, EARLY + 1):
+        pyramid(k, k + 1, tiles - k - 1)
+    take_cols()
+    relay()
+    for m in range(own // TILE):
+        for s in (2, 3):
+            sent(functools.partial(col_copy, m), s)
+    for k in range(1, EARLY + 1):
+        pyramid(k, 0, k + 1)
+        pyramid(k, tiles - k - 1, tiles)
+    take_ints()
+    take_rows(0)
+    for k in range(EARLY + 1, d + 1):
         pyramid(k)
-    take_rows(0)
-    for k in range(5, 9):
-        pyramid(k)
+    take_rows(1)
     for s in (2, 3):
         arrived(functools.partial(flat_copy, 1), s)
     edge_cells([(0, groups)])
     zone(0)
-    take_rows(1)
-
-    def turn_out(i, carry):
-        tall = v[d + i, PAD + d:PAD + d + w].T
-        out_ref[pl.ds(i, c, stride=h), :] = tall[:c]
-        out_ref[pl.ds(h - 1 - i, c, stride=h), :] = tall[c:]
-        return carry
-
-    lax.fori_loop(d, own, turn_out, 0, unroll=8)
+
     zone(1)
-    lax.fori_loop(0, d, turn_out, 0, unroll=8)
+    for i in range(d):
+        turn_out(i)
     for s in range(2):
         for n in range(3):
             sent(functools.partial(int_copy, n), s)
@@ -348,6 +406,7 @@
     for s in (2, 3):
         for late in range(2):
             sent(functools.partial(flat_copy, late), s)
+    relayed()
 
 
 def per_device(n_row, n_col, fire_state, fuel_class, firebreak, ignition, spread_rate, spread_rows, spread_cols, reaction, ignition_heat):
@@ -379,10 +438,12 @@
             pltpu.VMEM((2 * two, 2 * two), BF16),
             pltpu.VMEM((2 * (k8 + 8), 3 * two), F32),
             pltpu.VMEM((2, d, c, w), F32),
+            pltpu.VMEM((d - CHUNK, c, w), F32),
             pltpu.VMEM((2, groups + 1, 8, w), F32),
             pltpu.VMEM((2, groups + 1, 8, w), F32),
-            dma((d, 2)), dma((d, 2)), dma((3, 2)), dma((3, 2)), dma((2, 2)), dma((2, 2)), dma((2, 2)), dma((2, 2)),
+            dma((d, 2)), dma((d, 2)), dma((3, 2)), dma((3, 2)), dma((own // TILE, 2)), dma((own // TILE, 2)), dma((2, 2)), dma((2, 2)),
             dma((d // CHUNK, 2)), dma((d // CHUNK, 2)),
+            dma((d - CHUNK,)), dma((d - CHUNK,)),
         ],
         compiler_params=pltpu.CompilerParams(collective_id=0, has_side_effects=True, vmem_limit_bytes=56 * 1048576),
     )(

time: 26.9 us -> 23.7 us (0.88)
  Pallas kernels: 25.6 us -> 22.4 us
    pallas_call x1, Pallas kernels: 25.6 us -> 22.4 us  [per_device(): pl.pallas_call(functools.partial(kernel, (n_row, n_col, c, h, w, k8)), ou...]
where the time goes in v3:
time: 23.7 us; the launch traced here: 23.5 us
  Pallas kernels  22.4 us (95%)
  local copies, waits for them, and re-layouts  1.15 us (5%)
    pallas_call x1, Pallas kernels, per_device(): pl.pallas_call(functools.partial(kernel, (n_row, n_col, c, h, w, k8)), ou...  22.4 us
    unnamed x1, local copies, waits for them, and re-layouts  1.15 us

profile of v3, /device:TPU:1, one launch (start us, length us, event | category | flops | bytes accessed | tf_op | source)
XLA Modules:
  0.0 23.5 jit_solution(10855343453801286437)
XLA Ops:
  0.0 22.4 %shard_map.91 = f32[3072,128]{1,0:T(8,128)S(1)} custom-call(f32[64,48,128]{2,1,0:T(8,128)} %x_hbm.1, s32[48,128]{1,0:T(8,128)} %fuel_hbm.1, s32[48,128]{1,0:T(8,128)} %break_hbm.1, s32[48,128]{1,0:T(8,128)} %lit_hbm.1, f32[13,64]{1,0:T(8,128)} %rate_hbm.1, f32[64,64]{1,0:T(8,128)} %srow_hbm.1, f32[64,64]{1,0:T(8,128)} %scol_hbm.1, f32[64,64]{1,0:T(8,128)} %react_hbm.1, ...), custom_call_target="tpu_custom_call" | custom-call | tf_op jit(solution)/shard_map/pallas_call | solution.py:424
  22.4 1.1 %copy.11 = f32[64,48,128]{2,1,0:T(8,128)} copy(f32[64,48,128]{2,1,0:T(8,128)S(1)} %bitcast.2) | data formatting | bytes 3145728

commit v4 on v3

--- a/solution.py
+++ b/solution.py
@@ -12,7 +12,7 @@
 PAD = 8
 TILE = 8
 LARGEST = 72
-EARLY = 3
+EARLY = 4
 CHUNK = 4
 BF16, F32 = jnp.bfloat16, jnp.float32
 ROUND = 1.5 * 2.0 ** 15
@@ -377,6 +377,7 @@
 
     for k in range(1, EARLY + 1):
         pyramid(k, k + 1, tiles - k - 1)
+    take_ints()
     take_cols()
     relay()
     for m in range(own // TILE):
@@ -385,14 +386,14 @@
     for k in range(1, EARLY + 1):
         pyramid(k, 0, k + 1)
         pyramid(k, tiles - k - 1, tiles)
-    take_ints()
     take_rows(0)
-    for k in range(EARLY + 1, d + 1):
-        pyramid(k)
-    take_rows(1)
     for s in (2, 3):
         arrived(functools.partial(flat_copy, 1), s)
     edge_cells([(0, groups)])
+    for k in range(EARLY + 1, d + 1):
+        pyramid(k)
+        if k == d - 1:
+            take_rows(1)
     zone(0)
 
     zone(1)

time: 23.7 us -> 22.7 us (0.958)
  Pallas kernels: 22.4 us -> 21.3 us
    pallas_call x1, Pallas kernels: 22.4 us -> 21.3 us  [per_device(): pl.pallas_call(functools.partial(kernel, (n_row, n_col, c, h, w, k8)), ou...]
where the time goes in v4:
time: 22.7 us; the launch traced here: 22.4 us
  Pallas kernels  21.3 us (94%)
  local copies, waits for them, and re-layouts  1.15 us (5%)
    pallas_call x1, Pallas kernels, per_device(): pl.pallas_call(functools.partial(kernel, (n_row, n_col, c, h, w, k8)), ou...  21.3 us
    unnamed x1, local copies, waits for them, and re-layouts  1.15 us

profile of v4, /device:TPU:1, one launch (start us, length us, event | category | flops | bytes accessed | tf_op | source)
XLA Modules:
  0.0 22.4 jit_solution(11969513672668635531)
XLA Ops:
  0.0 21.3 %shard_map.91 = f32[3072,128]{1,0:T(8,128)S(1)} custom-call(f32[64,48,128]{2,1,0:T(8,128)} %x_hbm.1, s32[48,128]{1,0:T(8,128)} %fuel_hbm.1, s32[48,128]{1,0:T(8,128)} %break_hbm.1, s32[48,128]{1,0:T(8,128)} %lit_hbm.1, f32[13,64]{1,0:T(8,128)} %rate_hbm.1, f32[64,64]{1,0:T(8,128)} %srow_hbm.1, f32[64,64]{1,0:T(8,128)} %scol_hbm.1, f32[64,64]{1,0:T(8,128)} %react_hbm.1, ...), custom_call_target="tpu_custom_call" | custom-call | tf_op jit(solution)/shard_map/pallas_call | solution.py:425
  21.3 1.1 %copy.11 = f32[64,48,128]{2,1,0:T(8,128)} copy(f32[64,48,128]{2,1,0:T(8,128)S(1)} %bitcast.2) | data formatting | bytes 3145728
